TPU v7x, 32 devices: a whole 2x2x4 slice. The times are simulated.
32 devices in a mesh: dp: 2 (over x), ep2: 4 (over z), ep: 4 (over y, core).
Axes of the slice: x: 2, y: 2, z: 4, core: 2. Of those that a mesh axis runs over, the one named last changes fastest.
Arguments:
- tokens: bfloat16 [4096, 2560], P(('dp', 'ep2', 'ep')), parts along dimension 0
- expert_idx: int32 [4096, 6], P(('dp', 'ep2', 'ep')), parts along dimension 0
- gates: float32 [4096, 6], P(('dp', 'ep2', 'ep')), parts along dimension 0
- w_gate: bfloat16 [64, 2560, 1536], P(('ep2', 'ep'))
- w_up: bfloat16 [64, 2560, 1536], P(('ep2', 'ep'))
- w_down: bfloat16 [64, 1536, 2560], P(('ep2', 'ep'))
Outputs:
- output: bfloat16 [4096, 2560], P(('dp', 'ep2', 'ep')), parts along dimension 0
There are 2 independent parts. A program takes and returns all parts, laid end to end along the dimension named above; an argument that names none is the same for every part.
All inputs are finite; a program needn't handle non-finite values.
Results may differ from a plain program's by a relative error of at most 0.001.
Values are sent between devices in bfloat16 or wider.
A program may use at most 1 GiB of HBM per device.

v0:
```python
import functools

import jax
import jax.numpy as jnp
from jax import lax
from jax.experimental import pallas as pl
from jax.experimental.pallas import tpu as pltpu
from jax.sharding import PartitionSpec as P

MESH = pl.DeviceIdType.MESH
BF = jnp.bfloat16
F32 = jnp.float32
NZ = 4
NE = 4
NDEV = NZ * NE
LE = 4
CAP = 12
BLK = LE * CAP
PLANE = NE * BLK
HALF = BLK // 2
WINDOWS = (0, 8, 24, 32)
FC = 512
DC = 512
NG = 5
ND = 6


def iota(shape, dim):
    return lax.broadcasted_iota(jnp.int32, shape, dim)


def div_cap(v):
    return (v * 43691) >> 19


def piece(e, desc):
    base = (e // 2) * HALF
    if desc:
        return (base + 16, 8) if e % 2 else (base, 16)
    return (base + 8, 16) if e % 2 else (base, 8)


def kernel(tok, idx, gates, wg, wu, wd, out, xl, idxl, sel, xr, a_buf, h_buf, ys, yr, gm, acc, gu, wdb,
           gsem, dsem, isend, irecv, lsend, lrecv, ssend, srecv, ysend, yrecv):
    T, D = tok.shape
    F = wg.shape[2]
    n_f, n_d = F // FC, D // DC
    dp, z, ep = lax.axis_index("dp"), lax.axis_index("ep2"), lax.axis_index("ep")
    me = z * NE + ep
    low = z < NZ // 2
    inner = (z == 1) | (z == 2)
    near = jnp.where(low, 1 - z, 5 - z)
    far1 = jnp.where(low, 2, 1)
    far2 = jnp.where(low, 3, 0)

    def remote(src, dst, ss, rs, zz, ee):
        return pltpu.make_async_remote_copy(
            src_ref=src, dst_ref=dst, send_sem=ss, recv_sem=rs, device_id=(dp, zz, ee), device_id_type=MESH
        )

    def gu_copies(i):
        e, c, slot = lax.div(i, n_f), lax.rem(i, n_f), lax.rem(i, NG)
        cols = pl.ds(pl.multiple_of(c * FC, FC), FC)
        return (
            pltpu.make_async_copy(wg.at[e, :, cols], gu.at[slot, 0], gsem.at[slot, 0]),
            pltpu.make_async_copy(wu.at[e, :, cols], gu.at[slot, 1], gsem.at[slot, 1]),
        )

    def d_copies(i):
        e, c, slot = lax.div(i, n_d), lax.rem(i, n_d), lax.rem(i, ND)
        cols = pl.ds(pl.multiple_of(c * DC, DC), DC)
        return (pltpu.make_async_copy(wd.at[e, :, cols], wdb.at[slot], dsem.at[slot]),)

    for i in range(NG):
        for cp in gu_copies(jnp.int32(i)):
            cp.start()
    for i in range(ND):
        for cp in d_copies(jnp.int32(i)):
            cp.start()

    barrier = pltpu.get_barrier_semaphore()
    for k in range(1, NDEV):
        peer = lax.rem(me + k, NDEV)
        pl.semaphore_signal(barrier, inc=1, device_id=(dp, lax.div(peer, NE), lax.rem(peer, NE)), device_id_type=MESH)
    pl.semaphore_wait(barrier, NDEV - 1)

    def line(b, n, to):
        return remote(xl.at[b], xl.at[b], lsend.at[n], lrecv.at[b], to, ep)

    def line_own(n, to):
        return remote(tok, xl.at[z], lsend.at[n], lrecv.at[z], to, ep)

    def line_wait(b):
        line(b, 0, z).wait_recv()

    def icopy(k):
        return remote(idx, idxl.at[z], isend.at[k - 1], irecv.at[z], lax.rem(z + k, NZ), ep)

    @pl.when(inner)
    def _():
        line_own(0, far1).start()

    line_own(1, near).start()
    for k in range(1, NZ):
        icopy(k).start()
    idxl[z] = idx[...]
    xl[z] = tok[...]

    upper = jnp.where(iota((T, T), 0) < iota((T, T), 1), 1.0, 0.0).astype(BF)

    def codes(ids, first, n):
        eid = iota((n, T), 0) + first
        hit = jnp.zeros((n, T), F32)
        for j in range(6):
            hit = hit + jnp.where(ids[j : j + 1, :] == eid, 1.0, 0.0)
        rank = jnp.dot(hit.astype(BF), upper, preferred_element_type=F32)
        return jnp.where(hit > 0.5, rank, -1.0).astype(BF)

    def s_copy(b, k):
        d = lax.rem(ep + k, NE)
        return remote(sel.at[b, d], xr.at[b * NE + ep], ssend.at[b, k - 1], srecv.at[b * NE + ep], z, d)

    def select(b):
        code = codes(idxl[b], z * NE * LE, NE * LE)
        r = iota((PLANE, NE * LE), 0)
        ex = jnp.where(div_cap(r) == iota((PLANE, NE * LE), 1), 1.0, 0.0).astype(BF)
        code_r = jnp.dot(ex, code, preferred_element_type=F32)
        r = iota((PLANE, T), 0)
        slot = (r - div_cap(r) * CAP).astype(F32)
        pick = jnp.where(code_r == slot, 1.0, 0.0).astype(BF)

        def cols(c, _):
            cs = pl.ds(pl.multiple_of(c * DC, DC), DC)
            rows = jnp.dot(pick, xl[b, :, cs], preferred_element_type=F32).astype(BF)
            sel[b, :, :, cs] = rows.reshape(NE, BLK, DC)
            return 0

        lax.fori_loop(0, n_d, cols, 0)
        for k in range(1, NE):
            s_copy(b, k).start()
        xr[b * NE + ep] = sel[b, ep]

    def idx_wait(b):
        remote(idx, idxl.at[b], isend.at[0], irecv.at[b], z, ep).wait_recv()

    select(z)

    n_exp = NDEV * LE
    idx_v, gates_v = idx[...], gates[...]
    code = codes(idx_v, 0, n_exp)
    eid = iota((n_exp, T), 0)
    gate = jnp.zeros((n_exp, T), F32)
    for j in range(6):
        gate = gate + jnp.where(idx_v[j : j + 1, :] == eid, gates_v[j : j + 1, :], 0.0)
    g_hi = gate.astype(BF)
    rest = gate - g_hi.astype(F32)
    g_mid = rest.astype(BF)
    g_lo = (rest - g_mid.astype(F32)).astype(BF)

    def spread(a, ex):
        return lax.dot_general(a, ex, (((0,), (0,)), ((), ())), preferred_element_type=F32)

    for b in range(NZ):
        c = iota((n_exp, PLANE), 1)
        ex = jnp.where(div_cap(c) + b * NE * LE == iota((n_exp, PLANE), 0), 1.0, 0.0).astype(BF)
        c = iota((T, PLANE), 1)
        slot = (c - div_cap(c) * CAP).astype(F32)
        on = spread(code, ex) == slot
        for q, part in enumerate((g_hi, g_mid, g_lo)):
            gm[q, b] = jnp.where(on, spread(part, ex), 0.0).astype(BF)

    def pick_plane(a, b):
        return jnp.where(inner, a, b)

    q0, q1, q2 = pick_plane(far1, near), pick_plane(far2, far1), pick_plane(near, far2)
    line_wait(q0)

    @pl.when(inner)
    def _():
        line(far1, 2, near).start()
        line_wait(near)
        line(near, 3, far1).start()

    idx_wait(q0)
    select(q0)
    line_wait(q1)

    @pl.when(inner)
    def _():
        line(far2, 4, near).start()

    idx_wait(q1)
    select(q1)

    def rows_wait(b):
        for k in range(1, NE):
            i = b * NE + lax.rem(ep + k, NE)
            remote(xr.at[i], xr.at[i], ssend.at[0, 0], srecv.at[i], z, ep).wait_recv()

    def y_copy(zz, ee, e, desc):
        m = zz * NE + ee
        rows = pl.ds(*piece(e, desc))
        return remote(ys.at[m, rows], yr.at[me, rows], ysend.at[e, m], yrecv.at[e, me], zz, ee)

    def experts(p0, p1, n_pass):
        desc = n_pass == 1
        rows_wait(p0)

        @pl.when(p1 != p0)
        def _():
            rows_wait(p1)

        def step(i, ring, total, copies, before):
            if before:
                if n_pass == 0:
                    for cp in copies(i):
                        cp.wait()
                else:
                    @pl.when(i < total - ring if desc else i >= ring)
                    def _():
                        for cp in copies(i):
                            cp.wait()
            else:
                nxt = i - ring if desc else i + ring

                @pl.when(nxt >= 0 if desc else nxt < total)
                def _():
                    for cp in copies(nxt):
                        cp.start()

        for e in reversed(range(LE)) if desc else range(LE):
            win = WINDOWS[e]
            for s, p in enumerate((p0, p1)):
                def gather(m, _, s=s, p=p):
                    rows = pl.ds(pl.multiple_of(s * NE * 16 + m * 16, 16), 16)
                    a_buf[rows, :] = xr[p * NE + m, win : win + 16, :]
                    return 0

                lax.fori_loop(0, NE, gather, 0)

            def gate_up(c, _):
                c = n_f - 1 - c if desc else c
                i = e * n_f + c
                slot = lax.rem(i, NG)
                step(i, NG, LE * n_f, gu_copies, True)
                a = a_buf[...]
                g = jnp.dot(a, gu[slot, 0], preferred_element_type=F32)
                u = jnp.dot(a, gu[slot, 1], preferred_element_type=F32)
                h_buf[:, pl.ds(pl.multiple_of(c * FC, FC), FC)] = (jax.nn.silu(g) * u).astype(BF)
                step(i, NG, LE * n_f, gu_copies, False)
                return 0

            lax.fori_loop(0, n_f, gate_up, 0)

            def down_proj(c, _):
                c = n_d - 1 - c if desc else c
                i = e * n_d + c
                slot = lax.rem(i, ND)
                step(i, ND, LE * n_d, d_copies, True)
                y = jnp.dot(h_buf[...], wdb[slot], preferred_element_type=F32).reshape(2, NE, 16, DC)
                cs = pl.ds(pl.multiple_of(c * DC, DC), DC)
                second = (e % 2 == 0) == desc
                for s, p in enumerate((p0, p1)):
                    to = pl.ds(p * NE, NE)
                    if not second:
                        ys[to, win : win + 16, cs] = y[s].astype(BF)
                    elif e % 2:
                        old = ys[to, win : win + 8, cs].astype(F32)
                        keep = iota((NE, 8, DC), 1) < 4
                        ys[to, win : win + 8, cs] = jnp.where(keep, old, y[s, :, :8]).astype(BF)
                        ys[to, win + 8 : win + 16, cs] = y[s, :, 8:].astype(BF)
                    else:
                        old = ys[to, win + 8 : win + 16, cs].astype(F32)
                        keep = iota((NE, 8, DC), 1) >= 4
                        ys[to, win + 8 : win + 16, cs] = jnp.where(keep, old, y[s, :, 8:]).astype(BF)
                        ys[to, win : win + 8, cs] = y[s, :, :8].astype(BF)
                step(i, ND, LE * n_d, d_copies, False)
                return 0

            lax.fori_loop(0, n_d, down_proj, 0)

            @pl.when(p1 != p0)
            def _():
                for k in range(NE):
                    y_copy(p1, k, e, desc).start()

            for k in range(NE):
                @pl.when((p0 != z) | (k != ep))
                def _(k=k):
                    y_copy(p0, k, e, desc).start()

    experts(pick_plane(far1, z), pick_plane(far1, near), 0)

    @pl.when(jnp.logical_not(inner))
    def _():
        line_wait(q2)

    idx_wait(q2)
    select(q2)
    experts(pick_plane(far2, far1), pick_plane(far2, far1), 1)
    experts(pick_plane(z, far2), pick_plane(near, far2), 2)

    yr[me] = ys[me]

    def y_wait(i, desc):
        for e in range(LE):
            rows = pl.ds(*piece(e, desc))
            remote(yr.at[i, rows], yr.at[i, rows], ysend.at[0, 0], yrecv.at[e, i], z, ep).wait_recv()

    for n, b in enumerate((z, near, far1, far2)):
        second = jnp.abs(b - z) == 2
        for k in range(1 if n == 0 else 0, NE):
            i = b * NE + (lax.rem(ep + k, NE) if n == 0 else k)
            if n < 2:
                y_wait(i, False)
            else:
                @pl.when(second)
                def _(i=i):
                    y_wait(i, True)

                @pl.when(jnp.logical_not(second))
                def _(i=i):
                    y_wait(i, False)

        def mix(c, _):
            cs = pl.ds(pl.multiple_of(c * DC, DC), DC)
            rows = yr[pl.ds(b * NE, NE), :, cs].reshape(PLANE, DC)
            s = tok[:, cs].astype(F32) if n == 0 else acc[:, cs]
            for q in range(3):
                s = s + jnp.dot(gm[q, b], rows, preferred_element_type=F32)
            if n < NZ - 1:
                acc[:, cs] = s
            else:
                out[:, cs] = s.astype(BF)
            return 0

        lax.fori_loop(0, n_d, mix, 0)

    for k in range(1, NZ):
        icopy(k).wait_send()
    for b in range(NZ):
        for k in range(1, NE):
            s_copy(b, k).wait_send()
    line_own(1, near).wait_send()

    @pl.when(inner)
    def _():
        line_own(0, far1).wait_send()
        line(far1, 2, near).wait_send()
        line(near, 3, far1).wait_send()
        line(far2, 4, near).wait_send()

    for b in (z, near, far1, far2):
        second = jnp.abs(b - z) == 2
        for k in range(NE):
            for desc in (False, True):
                @pl.when((second if desc else jnp.logical_not(second)) & ((b != z) | (k != ep)))
                def _(b=b, k=k, desc=desc):
                    for e in range(LE):
                        y_copy(b, k, e, desc).wait_send()


def solution(mesh):
    row_spec = P(('dp', 'ep2', 'ep'), None)
    weight_spec = P(('ep2', 'ep'), None, None)

    def local_step(tokens, expert_idx, gates, w_gate, w_up, w_down):
        T, D = tokens.shape
        F = w_gate.shape[2]
        vm = pl.BlockSpec(memory_space=pltpu.VMEM)
        hbm = pl.BlockSpec(memory_space=pl.ANY)
        dma = pltpu.SemaphoreType.DMA
        return pl.pallas_call(
            kernel,
            name="moe",
            out_shape=jax.ShapeDtypeStruct((T, D), BF),
            in_specs=[vm, vm, vm, hbm, hbm, hbm],
            out_specs=vm,
            scratch_shapes=[
                pltpu.VMEM((NZ, T, D), BF),
                pltpu.VMEM((NZ, 6, T), jnp.int32),
                pltpu.VMEM((NZ, NE, BLK, D), BF),
                pltpu.VMEM((NDEV, BLK, D), BF),
                pltpu.VMEM((2 * NE * 16, D), BF),
                pltpu.VMEM((2 * NE * 16, F), BF),
                pltpu.VMEM((NDEV, BLK, D), BF),
                pltpu.VMEM((NDEV, BLK, D), BF),
                pltpu.VMEM((3, NZ, T, PLANE), BF),
                pltpu.VMEM((T, D), F32),
                pltpu.VMEM((NG, 2, D, FC), BF),
                pltpu.VMEM((ND, F, DC), BF),
                dma((NG, 2)),
                dma((ND,)),
                dma((NZ - 1,)),
                dma((NZ,)),
                dma((5,)),
                dma((NZ,)),
                dma((NZ, NE - 1)),
                dma((NDEV,)),
                dma((LE, NDEV)),
                dma((LE, NDEV)),
            ],
            compiler_params=pltpu.CompilerParams(
                collective_id=0, has_side_effects=True, vmem_limit_bytes=67043328
            ),
        )(tokens, expert_idx.T, gates.T, w_gate, w_up, w_down)

    return jax.shard_map(local_step, mesh=mesh, in_specs=(row_spec, row_spec, row_spec, weight_spec, weight_spec, weight_spec), out_specs=row_spec, check_vma=False)
```

profile of v0, /device:TPU:0, one launch (start us, length us, event | category | flops | bytes accessed | tf_op | source)
XLA Modules:
  0.0 158.9 jit_solution(5799792013942900712)
XLA Ops:
  0.0 156.9 %moe.1 = bf16[128,2560]{1,0:T(8,128)(2,1)} custom-call(bf16[128,2560]{1,0:T(8,128)(2,1)} %tok.1, s32[6,128]{1,0:T(8,128)} %bitcast.2, f32[6,128]{1,0:T(8,128)} %bitcast.3, bf16[4,2560,1536]{2,1,0:T(8,128)(2,1)} %wg.1, bf16[4,2560,1536]{2,1,0:T(8,128)(2,1)} %wu.1, bf16[4,1536,2560]{2,1,0:T(8,128)(2,1)} %wd.1), custom_call_target="tpu_custom_call" | custom-call | tf_op jit(solution)/shard_map/moe/pallas_call | solution.py:373
  156.9 2.0 %copy.8 = bf16[128,2560]{1,0:T(8,128)(2,1)} copy(bf16[128,2560]{1,0:T(8,128)(2,1)} %moe.1) | data formatting | bytes 1310720
where the time goes:
time: 161 us; the launch traced here: 159 us
  Pallas kernels  157 us (98%)
  local copies, waits for them, and re-layouts  1.97 us (1%)
    pallas_call x1, Pallas kernels, local_step(): pl.pallas_call(kernel, name='moe', out_shape=jax.ShapeDtypeStruct((T, D),...  157 us

commit v1 on v0

--- a/solution.py
+++ b/solution.py
@@ -192,6 +192,16 @@
     idx_wait(q1)
     select(q1)
 
+    def last_block():
+        @pl.when(jnp.logical_not(inner))
+        def _():
+            line_wait(q2)
+
+        idx_wait(q2)
+        select(q2)
+
+    pl.when(inner)(last_block)
+
     def rows_wait(b):
         for k in range(1, NE):
             i = b * NE + lax.rem(ep + k, NE)
@@ -205,10 +215,7 @@
     def experts(p0, p1, n_pass):
         desc = n_pass == 1
         rows_wait(p0)
-
-        @pl.when(p1 != p0)
-        def _():
-            rows_wait(p1)
+        rows_wait(p1)
 
         def step(i, ring, total, copies, before):
             if before:
@@ -279,26 +286,20 @@
 
             lax.fori_loop(0, n_d, down_proj, 0)
 
-            @pl.when(p1 != p0)
-            def _():
+            for k in range(NE):
+                y_copy(p0, k, e, desc).start()
+            if n_pass:
                 for k in range(NE):
                     y_copy(p1, k, e, desc).start()
-
-            for k in range(NE):
-                @pl.when((p0 != z) | (k != ep))
-                def _(k=k):
-                    y_copy(p0, k, e, desc).start()
-
-    experts(pick_plane(far1, z), pick_plane(far1, near), 0)
-
-    @pl.when(jnp.logical_not(inner))
-    def _():
-        line_wait(q2)
-
-    idx_wait(q2)
-    select(q2)
-    experts(pick_plane(far2, far1), pick_plane(far2, far1), 1)
-    experts(pick_plane(z, far2), pick_plane(near, far2), 2)
+            elif e == LE - 2:
+                pl.when(jnp.logical_not(inner))(last_block)
+        if n_pass == 0:
+            for e in range(LE):
+                for k in range(1, NE):
+                    y_copy(z, lax.rem(ep + k, NE), e, desc).start()
+
+    experts(pick_plane(far1, near), z, 0)
+    experts(far2, pick_plane(near, far1), 1)
 
     yr[me] = ys[me]
 
@@ -307,18 +308,18 @@
             rows = pl.ds(*piece(e, desc))
             remote(yr.at[i, rows], yr.at[i, rows], ysend.at[0, 0], yrecv.at[e, i], z, ep).wait_recv()
 
+    edge = jnp.logical_not(inner)
     for n, b in enumerate((z, near, far1, far2)):
-        second = jnp.abs(b - z) == 2
         for k in range(1 if n == 0 else 0, NE):
             i = b * NE + (lax.rem(ep + k, NE) if n == 0 else k)
-            if n < 2:
-                y_wait(i, False)
+            if n in (0, 3):
+                y_wait(i, n == 3)
             else:
-                @pl.when(second)
+                @pl.when(edge)
                 def _(i=i):
                     y_wait(i, True)
 
-                @pl.when(jnp.logical_not(second))
+                @pl.when(inner)
                 def _(i=i):
                     y_wait(i, False)
 
@@ -350,14 +351,22 @@
         line(near, 3, far1).wait_send()
         line(far2, 4, near).wait_send()
 
-    for b in (z, near, far1, far2):
-        second = jnp.abs(b - z) == 2
-        for k in range(NE):
-            for desc in (False, True):
-                @pl.when((second if desc else jnp.logical_not(second)) & ((b != z) | (k != ep)))
-                def _(b=b, k=k, desc=desc):
-                    for e in range(LE):
-                        y_copy(b, k, e, desc).wait_send()
+    def sent(b, k, desc):
+        for e in range(LE):
+            y_copy(b, k, e, desc).wait_send()
+
+    for k in range(NE):
+        if k:
+            sent(z, lax.rem(ep + k, NE), False)
+        sent(far2, k, True)
+        for desc in (False, True):
+            @pl.when(inner)
+            def _(k=k, desc=desc):
+                sent(near if desc else far1, k, desc)
+
+            @pl.when(edge)
+            def _(k=k, desc=desc):
+                sent(far1 if desc else near, k, desc)
 
 
 def solution(mesh):

time: 161 us -> 149 us (0.925)
  Pallas kernels: 157 us -> 146 us
    pallas_call x1, Pallas kernels: 157 us -> 146 us  [local_step(): pl.pallas_call(kernel, name='moe', out_shape=jax.ShapeDtypeStruct((T, D),...]
where the time goes in v1:
time: 149 us; the launch traced here: 148 us
  Pallas kernels  146 us (98%)
  local copies, waits for them, and re-layouts  1.97 us (1%)
    pallas_call x1, Pallas kernels, local_step(): pl.pallas_call(kernel, name='moe', out_shape=jax.ShapeDtypeStruct((T, D),...  146 us

profile of v1, /device:TPU:0, one launch (start us, length us, event | category | flops | bytes accessed | tf_op | source)
XLA Modules:
  0.0 147.9 jit_solution(14027505477867754421)
XLA Ops:
  0.0 145.9 %moe.1 = bf16[128,2560]{1,0:T(8,128)(2,1)} custom-call(bf16[128,2560]{1,0:T(8,128)(2,1)} %tok.1, s32[6,128]{1,0:T(8,128)} %bitcast.2, f32[6,128]{1,0:T(8,128)} %bitcast.3, bf16[4,2560,1536]{2,1,0:T(8,128)(2,1)} %wg.1, bf16[4,2560,1536]{2,1,0:T(8,128)(2,1)} %wu.1, bf16[4,1536,2560]{2,1,0:T(8,128)(2,1)} %wd.1), custom_call_target="tpu_custom_call" | custom-call | tf_op jit(solution)/shard_map/moe/pallas_call | solution.py:382
  145.9 2.0 %copy.8 = bf16[128,2560]{1,0:T(8,128)(2,1)} copy(bf16[128,2560]{1,0:T(8,128)(2,1)} %moe.1) | data formatting | bytes 1310720

commit v2 on v1

--- a/solution.py
+++ b/solution.py
@@ -49,6 +49,7 @@
     me = z * NE + ep
     low = z < NZ // 2
     inner = (z == 1) | (z == 2)
+    edge = jnp.logical_not(inner)
     near = jnp.where(low, 1 - z, 5 - z)
     far1 = jnp.where(low, 2, 1)
     far2 = jnp.where(low, 3, 0)
@@ -193,7 +194,7 @@
     select(q1)
 
     def last_block():
-        @pl.when(jnp.logical_not(inner))
+        @pl.when(edge)
         def _():
             line_wait(q2)
 
@@ -288,18 +289,15 @@
 
             for k in range(NE):
                 y_copy(p0, k, e, desc).start()
-            if n_pass:
-                for k in range(NE):
+            for k in range(NE):
+                @pl.when((p1 != z) | (k != ep))
+                def _(k=k):
                     y_copy(p1, k, e, desc).start()
-            elif e == LE - 2:
-                pl.when(jnp.logical_not(inner))(last_block)
-        if n_pass == 0:
-            for e in range(LE):
-                for k in range(1, NE):
-                    y_copy(z, lax.rem(ep + k, NE), e, desc).start()
-
-    experts(pick_plane(far1, near), z, 0)
-    experts(far2, pick_plane(near, far1), 1)
+            if n_pass == 0 and e == LE - 2:
+                pl.when(edge)(last_block)
+
+    experts(pick_plane(far1, near), pick_plane(far2, z), 0)
+    experts(pick_plane(near, far2), pick_plane(z, far1), 1)
 
     yr[me] = ys[me]
 
@@ -308,20 +306,20 @@
             rows = pl.ds(*piece(e, desc))
             remote(yr.at[i, rows], yr.at[i, rows], ysend.at[0, 0], yrecv.at[e, i], z, ep).wait_recv()
 
-    edge = jnp.logical_not(inner)
+    late_in = (inner, edge, z < 0, z >= 0)
+    late_out = (inner, inner, edge, edge)
+
     for n, b in enumerate((z, near, far1, far2)):
         for k in range(1 if n == 0 else 0, NE):
             i = b * NE + (lax.rem(ep + k, NE) if n == 0 else k)
-            if n in (0, 3):
-                y_wait(i, n == 3)
-            else:
-                @pl.when(edge)
-                def _(i=i):
-                    y_wait(i, True)
-
-                @pl.when(inner)
-                def _(i=i):
-                    y_wait(i, False)
+
+            @pl.when(late_in[n])
+            def _(i=i):
+                y_wait(i, True)
+
+            @pl.when(jnp.logical_not(late_in[n]))
+            def _(i=i):
+                y_wait(i, False)
 
         def mix(c, _):
             cs = pl.ds(pl.multiple_of(c * DC, DC), DC)
@@ -351,22 +349,14 @@
         line(near, 3, far1).wait_send()
         line(far2, 4, near).wait_send()
 
-    def sent(b, k, desc):
-        for e in range(LE):
-            y_copy(b, k, e, desc).wait_send()
-
-    for k in range(NE):
-        if k:
-            sent(z, lax.rem(ep + k, NE), False)
-        sent(far2, k, True)
-        for desc in (False, True):
-            @pl.when(inner)
-            def _(k=k, desc=desc):
-                sent(near if desc else far1, k, desc)
-
-            @pl.when(edge)
-            def _(k=k, desc=desc):
-                sent(far1 if desc else near, k, desc)
+    for n, b in enumerate((z, near, far1, far2)):
+        for k in range(1 if n == 0 else 0, NE):
+            d = lax.rem(ep + k, NE) if n == 0 else k
+            for desc in (False, True):
+                @pl.when(late_out[n] if desc else jnp.logical_not(late_out[n]))
+                def _(b=b, d=d, desc=desc):
+                    for e in range(LE):
+                        y_copy(b, d, e, desc).wait_send()
 
 
 def solution(mesh):

time: 149 us -> 150 us (level)
  no operation moved by 1% of the time
where the time goes in v2:
time: 150 us; the launch traced here: 149 us
  Pallas kernels  147 us (98%)
  local copies, waits for them, and re-layouts  1.97 us (1%)
    pallas_call x1, Pallas kernels, local_step(): pl.pallas_call(kernel, name='moe', out_shape=jax.ShapeDtypeStruct((T, D),...  147 us

profile of v2, /device:TPU:0, one launch (start us, length us, event | category | flops | bytes accessed | tf_op | source)
XLA Modules:
  0.0 149.2 jit_solution(10305003496026590193)
XLA Ops:
  0.0 147.3 %moe.1 = bf16[128,2560]{1,0:T(8,128)(2,1)} custom-call(bf16[128,2560]{1,0:T(8,128)(2,1)} %tok.1, s32[6,128]{1,0:T(8,128)} %bitcast.2, f32[6,128]{1,0:T(8,128)} %bitcast.3, bf16[4,2560,1536]{2,1,0:T(8,128)(2,1)} %wg.1, bf16[4,2560,1536]{2,1,0:T(8,128)(2,1)} %wu.1, bf16[4,1536,2560]{2,1,0:T(8,128)(2,1)} %wd.1), custom_call_target="tpu_custom_call" | custom-call | tf_op jit(solution)/shard_map/moe/pallas_call | solution.py:372
  147.3 2.0 %copy.8 = bf16[128,2560]{1,0:T(8,128)(2,1)} copy(bf16[128,2560]{1,0:T(8,128)(2,1)} %moe.1) | data formatting | bytes 1310720

commit v3 on v2

--- a/solution.py
+++ b/solution.py
@@ -23,6 +23,7 @@
 DC = 512
 NG = 5
 ND = 6
+PARTS = 2
 
 
 def iota(shape, dim):
@@ -40,7 +41,7 @@
     return (base + 8, 16) if e % 2 else (base, 8)
 
 
-def kernel(tok, idx, gates, wg, wu, wd, out, xl, idxl, sel, xr, a_buf, h_buf, ys, yr, gm, acc, gu, wdb,
+def kernel(tok, idx, gates, wg, wu, wd, out, xl, idxl, sel, xr, a_buf, h_buf, ys, yr, gm, acc, pick, gu, wdb,
            gsem, dsem, isend, irecv, lsend, lrecv, ssend, srecv, ysend, yrecv):
     T, D = tok.shape
     F = wg.shape[2]
@@ -85,23 +86,28 @@
         pl.semaphore_signal(barrier, inc=1, device_id=(dp, lax.div(peer, NE), lax.rem(peer, NE)), device_id_type=MESH)
     pl.semaphore_wait(barrier, NDEV - 1)
 
-    def line(b, n, to):
-        return remote(xl.at[b], xl.at[b], lsend.at[n], lrecv.at[b], to, ep)
-
-    def line_own(n, to):
-        return remote(tok, xl.at[z], lsend.at[n], lrecv.at[z], to, ep)
-
-    def line_wait(b):
-        line(b, 0, z).wait_recv()
+    def span(h):
+        return pl.ds(h * (D // PARTS), D // PARTS)
+
+    def line(b, n, to, h):
+        at = xl.at[b, :, span(h)]
+        return remote(at, at, lsend.at[n, h], lrecv.at[b, h], to, ep)
+
+    def line_own(n, to, h):
+        return remote(tok.at[:, span(h)], xl.at[z, :, span(h)], lsend.at[n, h], lrecv.at[z, h], to, ep)
+
+    def line_wait(b, h):
+        line(b, 0, z, h).wait_recv()
 
     def icopy(k):
         return remote(idx, idxl.at[z], isend.at[k - 1], irecv.at[z], lax.rem(z + k, NZ), ep)
 
-    @pl.when(inner)
-    def _():
-        line_own(0, far1).start()
-
-    line_own(1, near).start()
+    for h in range(PARTS):
+        @pl.when(inner)
+        def _(h=h):
+            line_own(0, far1, h).start()
+
+        line_own(1, near, h).start()
     for k in range(1, NZ):
         icopy(k).start()
     idxl[z] = idx[...]
@@ -117,34 +123,42 @@
         rank = jnp.dot(hit.astype(BF), upper, preferred_element_type=F32)
         return jnp.where(hit > 0.5, rank, -1.0).astype(BF)
 
-    def s_copy(b, k):
+    def s_copy(b, k, h):
         d = lax.rem(ep + k, NE)
-        return remote(sel.at[b, d], xr.at[b * NE + ep], ssend.at[b, k - 1], srecv.at[b * NE + ep], z, d)
-
-    def select(b):
+        return remote(
+            sel.at[b, d, :, span(h)], xr.at[b * NE + ep, :, span(h)], ssend.at[b, k - 1, h],
+            srecv.at[b * NE + ep, h], z, d
+        )
+
+    def picks(b):
         code = codes(idxl[b], z * NE * LE, NE * LE)
         r = iota((PLANE, NE * LE), 0)
         ex = jnp.where(div_cap(r) == iota((PLANE, NE * LE), 1), 1.0, 0.0).astype(BF)
         code_r = jnp.dot(ex, code, preferred_element_type=F32)
         r = iota((PLANE, T), 0)
         slot = (r - div_cap(r) * CAP).astype(F32)
-        pick = jnp.where(code_r == slot, 1.0, 0.0).astype(BF)
+        pick[...] = jnp.where(code_r == slot, 1.0, 0.0).astype(BF)
+
+    def select(b, h):
+        wide = D // PARTS // 2
 
         def cols(c, _):
-            cs = pl.ds(pl.multiple_of(c * DC, DC), DC)
-            rows = jnp.dot(pick, xl[b, :, cs], preferred_element_type=F32).astype(BF)
-            sel[b, :, :, cs] = rows.reshape(NE, BLK, DC)
+            cs = pl.ds(pl.multiple_of(h * (D // PARTS) + c * wide, 128), wide)
+            rows = jnp.dot(pick[...], xl[b, :, cs], preferred_element_type=F32).astype(BF)
+            sel[b, :, :, cs] = rows.reshape(NE, BLK, wide)
             return 0
 
-        lax.fori_loop(0, n_d, cols, 0)
+        lax.fori_loop(0, 2, cols, 0)
         for k in range(1, NE):
-            s_copy(b, k).start()
-        xr[b * NE + ep] = sel[b, ep]
+            s_copy(b, k, h).start()
+        xr[b * NE + ep, :, span(h)] = sel[b, ep, :, span(h)]
 
     def idx_wait(b):
         remote(idx, idxl.at[b], isend.at[0], irecv.at[b], z, ep).wait_recv()
 
-    select(z)
+    picks(z)
+    for h in range(PARTS):
+        select(z, h)
 
     n_exp = NDEV * LE
     idx_v, gates_v = idx[...], gates[...]
@@ -174,39 +188,50 @@
         return jnp.where(inner, a, b)
 
     q0, q1, q2 = pick_plane(far1, near), pick_plane(far2, far1), pick_plane(near, far2)
-    line_wait(q0)
-
-    @pl.when(inner)
-    def _():
-        line(far1, 2, near).start()
-        line_wait(near)
-        line(near, 3, far1).start()
-
-    idx_wait(q0)
-    select(q0)
-    line_wait(q1)
-
-    @pl.when(inner)
-    def _():
-        line(far2, 4, near).start()
-
-    idx_wait(q1)
-    select(q1)
+    for h in range(PARTS):
+        line_wait(q0, h)
+
+        @pl.when(inner)
+        def _(h=h):
+            line(far1, 2, near, h).start()
+            line_wait(near, h)
+            line(near, 3, far1, h).start()
+
+        if h == 0:
+            idx_wait(q0)
+            picks(q0)
+        select(q0, h)
+
+    for h in range(PARTS):
+        if h == 0:
+            idx_wait(q1)
+            picks(q1)
+        line_wait(q1, h)
+
+        @pl.when(inner)
+        def _(h=h):
+            line(far2, 4, near, h).start()
+
+        select(q1, h)
 
     def last_block():
-        @pl.when(edge)
-        def _():
-            line_wait(q2)
-
         idx_wait(q2)
-        select(q2)
+        picks(q2)
+        for h in range(PARTS):
+            @pl.when(edge)
+            def _(h=h):
+                line_wait(q2, h)
+
+            select(q2, h)
 
     pl.when(inner)(last_block)
 
     def rows_wait(b):
         for k in range(1, NE):
             i = b * NE + lax.rem(ep + k, NE)
-            remote(xr.at[i], xr.at[i], ssend.at[0, 0], srecv.at[i], z, ep).wait_recv()
+            for h in range(PARTS):
+                at = xr.at[i, :, span(h)]
+                remote(at, at, ssend.at[0, 0, 0], srecv.at[i, h], z, ep).wait_recv()
 
     def y_copy(zz, ee, e, desc):
         m = zz * NE + ee
@@ -339,15 +364,17 @@
         icopy(k).wait_send()
     for b in range(NZ):
         for k in range(1, NE):
-            s_copy(b, k).wait_send()
-    line_own(1, near).wait_send()
-
-    @pl.when(inner)
-    def _():
-        line_own(0, far1).wait_send()
-        line(far1, 2, near).wait_send()
-        line(near, 3, far1).wait_send()
-        line(far2, 4, near).wait_send()
+            for h in range(PARTS):
+                s_copy(b, k, h).wait_send()
+    for h in range(PARTS):
+        line_own(1, near, h).wait_send()
+
+        @pl.when(inner)
+        def _(h=h):
+            line_own(0, far1, h).wait_send()
+            line(far1, 2, near, h).wait_send()
+            line(near, 3, far1, h).wait_send()
+            line(far2, 4, near, h).wait_send()
 
     for n, b in enumerate((z, near, far1, far2)):
         for k in range(1 if n == 0 else 0, NE):
@@ -386,16 +413,17 @@
                 pltpu.VMEM((NDEV, BLK, D), BF),
                 pltpu.VMEM((3, NZ, T, PLANE), BF),
                 pltpu.VMEM((T, D), F32),
+                pltpu.VMEM((PLANE, T), BF),
                 pltpu.VMEM((NG, 2, D, FC), BF),
                 pltpu.VMEM((ND, F, DC), BF),
                 dma((NG, 2)),
                 dma((ND,)),
                 dma((NZ - 1,)),
                 dma((NZ,)),
-                dma((5,)),
-                dma((NZ,)),
-                dma((NZ, NE - 1)),
-                dma((NDEV,)),
+                dma((5, PARTS)),
+                dma((NZ, PARTS)),
+                dma((NZ, NE - 1, PARTS)),
+                dma((NDEV, PARTS)),
                 dma((LE, NDEV)),
                 dma((LE, NDEV)),
             ],

time: 150 us -> 146 us (0.973)
  Pallas kernels: 147 us -> 142 us
    pallas_call x1, Pallas kernels: 147 us -> 142 us  [local_step(): pl.pallas_call(kernel, name='moe', out_shape=jax.ShapeDtypeStruct((T, D),...]
where the time goes in v3:
time: 146 us; the launch traced here: 144 us
  Pallas kernels  142 us (97%)
  local copies, waits for them, and re-layouts  1.97 us (1%)
    pallas_call x1, Pallas kernels, local_step(): pl.pallas_call(kernel, name='moe', out_shape=jax.ShapeDtypeStruct((T, D),...  142 us

profile of v3, /device:TPU:0, one launch (start us, length us, event | category | flops | bytes accessed | tf_op | source)
XLA Modules:
  0.0 144.5 jit_solution(6628991318624702252)
XLA Ops:
  0.0 142.5 %moe.1 = bf16[128,2560]{1,0:T(8,128)(2,1)} custom-call(bf16[128,2560]{1,0:T(8,128)(2,1)} %tok.1, s32[6,128]{1,0:T(8,128)} %bitcast.2, f32[6,128]{1,0:T(8,128)} %bitcast.3, bf16[4,2560,1536]{2,1,0:T(8,128)(2,1)} %wg.1, bf16[4,2560,1536]{2,1,0:T(8,128)(2,1)} %wu.1, bf16[4,1536,2560]{2,1,0:T(8,128)(2,1)} %wd.1), custom_call_target="tpu_custom_call" | custom-call | tf_op jit(solution)/shard_map/moe/pallas_call | solution.py:399
  142.5 2.0 %copy.8 = bf16[128,2560]{1,0:T(8,128)(2,1)} copy(bf16[128,2560]{1,0:T(8,128)(2,1)} %moe.1) | data formatting | bytes 1310720

commit v4 on v3

--- a/solution.py
+++ b/solution.py
@@ -314,15 +314,18 @@
 
             for k in range(NE):
                 y_copy(p0, k, e, desc).start()
-            for k in range(NE):
-                @pl.when((p1 != z) | (k != ep))
-                def _(k=k):
+            if n_pass:
+                for k in range(NE):
                     y_copy(p1, k, e, desc).start()
-            if n_pass == 0 and e == LE - 2:
+            elif e == LE - 2:
                 pl.when(edge)(last_block)
-
-    experts(pick_plane(far1, near), pick_plane(far2, z), 0)
-    experts(pick_plane(near, far2), pick_plane(z, far1), 1)
+        if n_pass == 0:
+            for e in range(LE):
+                for k in range(1, NE):
+                    y_copy(z, lax.rem(ep + k, NE), e, desc).start()
+
+    experts(pick_plane(far1, near), z, 0)
+    experts(far2, pick_plane(near, far1), 1)
 
     yr[me] = ys[me]
 
@@ -331,8 +334,8 @@
             rows = pl.ds(*piece(e, desc))
             remote(yr.at[i, rows], yr.at[i, rows], ysend.at[0, 0], yrecv.at[e, i], z, ep).wait_recv()
 
-    late_in = (inner, edge, z < 0, z >= 0)
-    late_out = (inner, inner, edge, edge)
+    late_in = (z < 0, edge, edge, z >= 0)
+    late_out = (z < 0, inner, edge, z >= 0)
 
     for n, b in enumerate((z, near, far1, far2)):
         for k in range(1 if n == 0 else 0, NE):

time: 146 us -> 147 us (level)
  the two profiles are of different devices: /device:TPU:0 before, /device:TPU:5 now
where the time goes in v4:
time: 147 us
  Pallas kernels  145 us (99%)
  local copies, waits for them, and re-layouts  1.97 us (1%)
    pallas_call x1, Pallas kernels, local_step(): pl.pallas_call(kernel, name='moe', out_shape=jax.ShapeDtypeStruct((T, D),...  145 us

profile of v4, /device:TPU:5, one launch (start us, length us, event | category | flops | bytes accessed | tf_op | source)
XLA Modules:
  0.0 147.1 jit_solution(5125622532001082514)
XLA Ops:
  0.0 145.1 %moe.1 = bf16[128,2560]{1,0:T(8,128)(2,1)} custom-call(bf16[128,2560]{1,0:T(8,128)(2,1)} %tok.1, s32[6,128]{1,0:T(8,128)} %bitcast.2, f32[6,128]{1,0:T(8,128)} %bitcast.3, bf16[4,2560,1536]{2,1,0:T(8,128)(2,1)} %wg.1, bf16[4,2560,1536]{2,1,0:T(8,128)(2,1)} %wu.1, bf16[4,1536,2560]{2,1,0:T(8,128)(2,1)} %wd.1), custom_call_target="tpu_custom_call" | custom-call | tf_op jit(solution)/shard_map/moe/pallas_call | solution.py:402
  145.1 2.0 %copy.8 = bf16[128,2560]{1,0:T(8,128)(2,1)} copy(bf16[128,2560]{1,0:T(8,128)(2,1)} %moe.1) | data formatting | bytes 1310720

commit v5 on v3

--- a/solution.py
+++ b/solution.py
@@ -232,6 +232,9 @@
             for h in range(PARTS):
                 at = xr.at[i, :, span(h)]
                 remote(at, at, ssend.at[0, 0, 0], srecv.at[i, h], z, ep).wait_recv()
+
+    def across(k):
+        return lax.rem(lax.div(ep, 2) + k // 2, 2) * 2 + lax.rem(lax.rem(ep, 2) + k % 2, 2)
 
     def y_copy(zz, ee, e, desc):
         m = zz * NE + ee
@@ -313,11 +316,14 @@
             lax.fori_loop(0, n_d, down_proj, 0)
 
             for k in range(NE):
-                y_copy(p0, k, e, desc).start()
+                y_copy(p0, across(k), e, desc).start()
             for k in range(NE):
-                @pl.when((p1 != z) | (k != ep))
-                def _(k=k):
-                    y_copy(p1, k, e, desc).start()
+                if k:
+                    y_copy(p1, across(k), e, desc).start()
+                else:
+                    @pl.when(p1 != z)
+                    def _():
+                        y_copy(p1, ep, e, desc).start()
             if n_pass == 0 and e == LE - 2:
                 pl.when(edge)(last_block)
 

time: 146 us -> 147 us (level)
  Pallas kernels: 142 us -> 145 us
    pallas_call x1, Pallas kernels: 142 us -> 145 us  [local_step(): pl.pallas_call(kernel, name='moe', out_shape=jax.ShapeDtypeStruct((T, D),...]
where the time goes in v5:
time: 147 us
  Pallas kernels  145 us (99%)
  local copies, waits for them, and re-layouts  1.97 us (1%)
    pallas_call x1, Pallas kernels, local_step(): pl.pallas_call(kernel, name='moe', out_shape=jax.ShapeDtypeStruct((T, D),...  145 us

profile of v5, /device:TPU:0, one launch (start us, length us, event | category | flops | bytes accessed | tf_op | source)
XLA Modules:
  0.0 146.8 jit_solution(6846570897472931069)
XLA Ops:
  0.0 144.8 %moe.1 = bf16[128,2560]{1,0:T(8,128)(2,1)} custom-call(bf16[128,2560]{1,0:T(8,128)(2,1)} %tok.1, s32[6,128]{1,0:T(8,128)} %bitcast.2, f32[6,128]{1,0:T(8,128)} %bitcast.3, bf16[4,2560,1536]{2,1,0:T(8,128)(2,1)} %wg.1, bf16[4,2560,1536]{2,1,0:T(8,128)(2,1)} %wu.1, bf16[4,1536,2560]{2,1,0:T(8,128)(2,1)} %wd.1), custom_call_target="tpu_custom_call" | custom-call | tf_op jit(solution)/shard_map/moe/pallas_call | solution.py:405
  144.8 2.0 %copy.8 = bf16[128,2560]{1,0:T(8,128)(2,1)} copy(bf16[128,2560]{1,0:T(8,128)(2,1)} %moe.1) | data formatting | bytes 1310720

commit v6 on v3

--- a/solution.py
+++ b/solution.py
@@ -73,6 +73,10 @@
         cols = pl.ds(pl.multiple_of(c * DC, DC), DC)
         return (pltpu.make_async_copy(wd.at[e, :, cols], wdb.at[slot], dsem.at[slot]),)
 
+    barrier = pltpu.get_barrier_semaphore()
+    for k in range(1, NDEV):
+        peer = lax.rem(me + k, NDEV)
+        pl.semaphore_signal(barrier, inc=1, device_id=(dp, lax.div(peer, NE), lax.rem(peer, NE)), device_id_type=MESH)
     for i in range(NG):
         for cp in gu_copies(jnp.int32(i)):
             cp.start()
@@ -80,10 +84,6 @@
         for cp in d_copies(jnp.int32(i)):
             cp.start()
 
-    barrier = pltpu.get_barrier_semaphore()
-    for k in range(1, NDEV):
-        peer = lax.rem(me + k, NDEV)
-        pl.semaphore_signal(barrier, inc=1, device_id=(dp, lax.div(peer, NE), lax.rem(peer, NE)), device_id_type=MESH)
     pl.semaphore_wait(barrier, NDEV - 1)
 
     def span(h):
@@ -232,6 +232,9 @@
             for h in range(PARTS):
                 at = xr.at[i, :, span(h)]
                 remote(at, at, ssend.at[0, 0, 0], srecv.at[i, h], z, ep).wait_recv()
+
+    def across(k):
+        return lax.rem(lax.div(ep, 2) + lax.rem(ep, 2) + k // 2, 2) * 2 + lax.rem(lax.rem(ep, 2) + k % 2, 2)
 
     def y_copy(zz, ee, e, desc):
         m = zz * NE + ee
@@ -313,11 +316,11 @@
             lax.fori_loop(0, n_d, down_proj, 0)
 
             for k in range(NE):
-                y_copy(p0, k, e, desc).start()
+                y_copy(p0, across(k), e, desc).start()
             for k in range(NE):
-                @pl.when((p1 != z) | (k != ep))
+                @pl.when((p1 != z) | (across(k) != ep))
                 def _(k=k):
-                    y_copy(p1, k, e, desc).start()
+                    y_copy(p1, across(k), e, desc).start()
             if n_pass == 0 and e == LE - 2:
                 pl.when(edge)(last_block)
 

time: 146 us -> 146 us (level); the launches traced: 144 us -> 146 us
  Pallas kernels: 142 us -> 144 us
    pallas_call x1, Pallas kernels: 142 us -> 144 us  [local_step(): pl.pallas_call(kernel, name='moe', out_shape=jax.ShapeDtypeStruct((T, D),...]
where the time goes in v6:
time: 146 us
  Pallas kernels  144 us (99%)
  local copies, waits for them, and re-layouts  1.97 us (1%)
    pallas_call x1, Pallas kernels, local_step(): pl.pallas_call(kernel, name='moe', out_shape=jax.ShapeDtypeStruct((T, D),...  144 us

profile of v6, /device:TPU:0, one launch (start us, length us, event | category | flops | bytes accessed | tf_op | source)
XLA Modules:
  0.0 146.1 jit_solution(5158818622991188604)
XLA Ops:
  0.0 144.1 %moe.1 = bf16[128,2560]{1,0:T(8,128)(2,1)} custom-call(bf16[128,2560]{1,0:T(8,128)(2,1)} %tok.1, s32[6,128]{1,0:T(8,128)} %bitcast.2, f32[6,128]{1,0:T(8,128)} %bitcast.3, bf16[4,2560,1536]{2,1,0:T(8,128)(2,1)} %wg.1, bf16[4,2560,1536]{2,1,0:T(8,128)(2,1)} %wu.1, bf16[4,1536,2560]{2,1,0:T(8,128)(2,1)} %wd.1), custom_call_target="tpu_custom_call" | custom-call | tf_op jit(solution)/shard_map/moe/pallas_call | solution.py:402
  144.1 2.0 %copy.8 = bf16[128,2560]{1,0:T(8,128)(2,1)} copy(bf16[128,2560]{1,0:T(8,128)(2,1)} %moe.1) | data formatting | bytes 1310720
